TPU v7x, 32 devices: a whole 2x2x4 slice. The times are simulated.
32 devices in a mesh: layer: 4 (over y, x), row: 2 (over core), col: 4 (over z).
Axes of the slice: x: 2, y: 2, z: 4, core: 2. Of those that a mesh axis runs over, the one named last changes fastest.
Arguments:
- hidden: bfloat16 [384, 2304], P(('layer', 'row')), may hold values from -60 to 60
- embedding: bfloat16 [16384, 2304], P(('row', 'col'), 'layer'), may hold values from -0.3 to 0.3
- teacher: bfloat16 [384, 16384], P('layer', ('row', 'col')), may hold values from -80 to 240
Outputs:
- grad_embedding: float32 [16384, 2304], P(('row', 'col'), 'layer')
- grad_hidden: float32 [384, 2304], P(('layer', 'row', 'col'))
All inputs are finite; a program needn't handle non-finite values.
Results may differ from a plain program's by a relative error of at most 0.0041.
Values may be sent and summed in bfloat16 or wider, within the bound.
A program may use at most 192 MiB of HBM per device.

v0:
```python
import jax
import jax.numpy as jnp
from jax import lax
from jax.sharding import PartitionSpec as P

LOSS_SCALE = 256


def local(hidden, embedding, teacher):
    token_rows = lax.all_gather(hidden, "row", axis=0, tiled=True)
    width_part = lax.all_to_all(token_rows, "layer", split_axis=1, concat_axis=0, tiled=True)
    logits = lax.psum_scatter(
        lax.dot_general(
            width_part, embedding, (((1,), (1,)), ((), ())), preferred_element_type=jnp.float32
        ),
        "layer",
        scatter_dimension=0,
        tiled=True,
    )
    teach_f = teacher.astype(jnp.float32)
    top_s, top_t = lax.pmax((jnp.max(logits, axis=1), jnp.max(teach_f, axis=1)), ("row", "col"))
    part_s = jnp.sum(jnp.exp(logits - top_s[:, None]), axis=1)
    part_t = jnp.sum(jnp.exp(teach_f - top_t[:, None]), axis=1)
    sum_s, sum_t = lax.psum((part_s, part_t), ("row", "col"))
    lse_s = top_s + jnp.log(sum_s)
    lse_t = top_t + jnp.log(sum_t)
    prob_s = jnp.exp(logits - lse_s[:, None])
    prob_t = jnp.exp(teach_f - lse_t[:, None])
    grads = ((prob_s - prob_t) * LOSS_SCALE).astype(jnp.bfloat16)
    grad_piece = lax.all_gather(grads, "layer", axis=0, tiled=True)
    embed_acc = lax.dot_general(
        grad_piece, width_part, (((0,), (0,)), ((), ())), preferred_element_type=jnp.float32
    )
    hidden_piece = jnp.dot(grad_piece, embedding, preferred_element_type=jnp.float32)
    hidden_terms = lax.all_to_all(hidden_piece, "layer", split_axis=0, concat_axis=1, tiled=True)
    grad_hidden = lax.psum_scatter(hidden_terms, ("row", "col"), scatter_dimension=0, tiled=True)
    return (embed_acc, grad_hidden)


def solution(mesh):
    placed = (P(("layer", "row"), None), P(("row", "col"), "layer"), P("layer", ("row", "col")))
    return jax.shard_map(
        local,
        mesh=mesh,
        in_specs=placed,
        out_specs=(P(("row", "col"), "layer"), P(("layer", "row", "col"), None)),
        check_vma=False,
    )
```

profile of v0, /device:TPU:1, one launch (start us, length us, event | category | flops | bytes accessed | tf_op | source)
XLA Modules:
  0.0 216.0 jit_solution(10763876937868347929)
XLA Ops:
  7.2 0.0 copy-start
  7.2 0.0 reduce-scatter.4.cloned.1.call-start
  7.2 2.5 %all_gather.6 = bf16[96,2304]{1,0:T(8,128)(2,1)S(1)} all-gather(bf16[48,2304]{1,0:T(8,128)(2,1)} %param.3), channel_id=1, replica_groups=mesh['layer'=4,'row'=2,'col'=4] {'row'}, dimensions={0}, use_global_device_ids=true | all-gather | bytes 663552 | tf_op jit(solution)/shard_map/all_gather | solution.py:10
  9.7 0.6 all_to_all.28
  10.3 0.1 copy.11
  10.3 11.5 %all_to_all.38 = bf16[96,4,576]{2,0,1:T(8,128)(2,1)S(1)} all-to-all(bf16[96,4,576]{2,0,1:T(8,128)(2,1)S(1)} %copy.11), channel_id=1, replica_groups=mesh['layer'=4,'row'=2,'col'=4] {'layer'}, dimensions={1} | all-to-all | bytes 884736 | tf_op jit(solution)/shard_map/all_to_all | solution.py:11
  21.8 0.0 copy-start.2
  21.8 0.8 copy-done.2
  22.6 0.0 copy-done
  22.6 3.1 %fusion.7 = f32[384,2048]{1,0:T(8,128)} fusion(bf16[384,576]{1,0:T(8,128)(2,1)S(1)} %bitcast.14, bf16[2048,576]{0,1:T(8,128)(2,1)S(1)} %copy-done), kind=kOutput, calls=%fused_computation.12 | convolution fusion | flops 905969664 | bytes 5947392 | tf_op jit(solution)/shard_map/dot_general | solution.py:13
  25.7 0.0 copy-start.5
  25.7 0.0 reduce-scatter.4.cloned.1.call-update
  25.7 0.0 all-gather.2.cloned.1.call-start
  25.8 0.9 copy-done.5
  26.7 0.2 reduce_max.24
  26.8 43.8 %reduce-scatter.4.cloned.1.call-done = f32[96,2048]{1,0:T(8,128)} async-done(((f32[384,2048]{1,0:T(8,128)}), f32[96,2048]{1,0:T(8,128)}) %reduce-scatter.4.cloned.1.call-update) | async-done | bytes 786448 | tf_op jit(solution)/shard_map/reduce_scatter | solution.py:12
  70.6 0.0 copy-start.1
  70.6 1.3 reduce_max.23
  72.0 17.8 %all-reduce.3 = (f32[96]{0:T(128)S(1)}, f32[96]{0:T(128)S(1)}) all-reduce(bf16[96]{0:T(256)(128)(2,1)S(1)} %reduce_max.24, f32[96]{0:T(128)S(1)} %reduce_max.23), channel_id=1, replica_groups=mesh['layer'=4,'row'=2,'col'=4] {'row','col'}, use_global_device_ids=true, to_apply=%region_6.0 | all-reduce | flops 192 | bytes 1344 | tf_op jit(solution)/shard_map/pmax | solution.py:21
  89.8 1.5 fusion.2
  91.4 14.2 %all-reduce.2 = (f32[96]{0:T(128)}, f32[96]{0:T(128)}) all-reduce(f32[96]{0:T(128)S(1)} %get-tuple-element.6, f32[96]{0:T(128)S(1)} %get-tuple-element.7), channel_id=1, replica_groups=mesh['layer'=4,'row'=2,'col'=4] {'row','col'}, use_global_device_ids=true, to_apply=%region_8.0 | all-reduce | flops 192 | bytes 1536 | tf_op jit(solution)/shard_map/psum | solution.py:24
  105.6 0.7 log_add_fusion
  106.2 0.7 log_add_fusion.1
  106.9 0.0 copy-done.1
  106.9 1.1 fusion.6
  108.0 0.0 all-gather.2.cloned.1.call-update
  108.0 0.0 copy-start.6
  108.0 29.8 %all-gather.2.cloned.1.call-done = bf16[384,2048]{1,0:T(8,128)(2,1)} async-done(((bf16[96,2048]{1,0:T(8,128)(2,1)}), bf16[384,2048]{1,0:T(8,128)(2,1)}) %all-gather.2.cloned.1.call-update) | async-done | bytes 1572880 | tf_op jit(solution)/shard_map/all_gather | solution.py:30
  137.8 3.8 %fusion.9 = f32[384,576]{1,0:T(8,128)} fusion(bf16[384,2048]{1,0:T(8,128)(2,1)} %all-gather.2.cloned.1.call-done, bf16[2048,576]{0,1:T(8,128)(2,1)S(1)} %copy-done), kind=kOutput, calls=%fused_computation.14 | convolution fusion | flops 905969664 | bytes 4816896 | tf_op jit(solution)/shard_map/dot_general | solution.py:34
  141.6 3.5 %all-to-all-start.1 = ((f32[4,96,576]{2,1,0:T(8,128)}), f32[4,96,576]{2,1,0:T(8,128)S(1)}, u32[]{:S(2)}, u32[]{:S(2)}) async-start(f32[4,96,576]{2,1,0:T(8,128)} %bitcast.17), calls=%async_computation.2 | async-start | bytes 1966080 | tf_op jit(solution)/shard_map/all_to_all | solution.py:35
  145.1 0.0 copy-done.6
  145.1 0.6 dynamic-slice.4
  146.3 11.2 %all-to-all-done.1 = f32[4,96,576]{2,1,0:T(8,128)S(1)} async-done(((f32[4,96,576]{2,1,0:T(8,128)}), f32[4,96,576]{2,1,0:T(8,128)S(1)}, u32[]{:S(2)}, u32[]{:S(2)}) %all-to-all-start.1) | async-done | bytes 884768 | tf_op jit(solution)/shard_map/all_to_all | solution.py:35
  157.5 0.0 copy-start.4
  157.5 0.9 copy-done.4
  158.4 0.0 copy-start.3
  158.4 2.8 %copy.13 = f32[96,4,576]{2,1,0:T(4,128)} copy(f32[96,4,576]{2,0,1:T(8,128)} %bitcast.16) | data formatting | bytes 1769472 | tf_op jit(solution)/shard_map/all_to_all | solution.py:35
  161.3 2.7 %all_to_all.35 = f32[96,2304]{1,0:T(8,128)} reshape(f32[96,4,576]{2,1,0:T(4,128)} %copy.13) | data formatting | bytes 1769472 | tf_op jit(solution)/shard_map/all_to_all | solution.py:35
  164.0 32.7 %fusion = f32[16,2304]{1,0:T(8,128)S(1)} fusion(f32[96,2304]{1,0:T(8,128)} %all_to_all.35), kind=kCustom, calls=%all-reduce-scatter | all-reduce-scatter fusion | flops 294913 | bytes 1032704
  196.7 1.9 collective-permute-start
  198.6 2.4 %collective-permute-start.1 = (f32[12,2304]{1,0:T(8,128)S(1)}, f32[12,2304]{1,0:T(8,128)S(1)}, u32[]{:S(2)}, u32[]{:S(2)}) collective-permute-start(f32[12,2304]{1,0:T(8,128)S(1)} %slice), channel_id=1, source_target_pairs={{0,2},{1,3},{2,4},{3,5},{4,6},{5,7},{8,10},{9,11},{10,12},{11,13},... | collective-permute-start | bytes 331784
  201.0 0.0 copy-done.3
  201.0 5.0 %fusion.8 = f32[2048,576]{0,1:T(8,128)} fusion(bf16[384,2048]{1,0:T(8,128)(2,1)} %all-gather.2.cloned.1.call-done, bf16[384,576]{1,0:T(8,128)(2,1)S(1)} %bitcast.15), kind=kOutput, calls=%fused_computation.13 | convolution fusion | flops 905969664 | bytes 6733824 | tf_op jit(solution)/shard_map/dot_general | solution.py:31
  206.1 2.0 collective-permute-done.1
  208.1 0.0 collective-permute-done
  208.1 0.4 concatenate
  208.5 0.7 constant_dynamic-slice_fusion
  (1 shorter events, 0.0 us)
Async XLA Ops:
  7.2 15.5 %copy-start = (bf16[2048,576]{0,1:T(8,128)(2,1)S(1)}, bf16[2048,576]{0,1:T(8,128)(2,1)}, u32[]{:S(2)}) copy-start(bf16[2048,576]{0,1:T(8,128)(2,1)} %param.4) | copy-start | bytes 7077892
  7.2 63.5 %reduce-scatter.4.cloned.1.call-start = ((), (), s32[]{:S(2)}) async-start(), calls=%async_computation.3 | async-start | bytes 3932160 | tf_op jit(solution)/shard_map/reduce_scatter | solution.py:12
  21.8 0.8 copy-start.2
  25.7 1.0 copy-start.5
  25.7 112.1 %all-gather.2.cloned.1.call-start = ((), (), s32[]{:S(2)}) async-start(), calls=%async_computation.4 | async-start | bytes 1966080 | tf_op jit(solution)/shard_map/all_gather | solution.py:30
  70.6 36.2 %copy-start.1 = (f32[96,2048]{1,0:T(8,128)S(1)}, f32[96,2048]{1,0:T(8,128)}, u32[]{:S(2)}) copy-start(f32[96,2048]{1,0:T(8,128)} %reduce-scatter.4.cloned.1.call-done) | copy-start | bytes 2359300
  108.0 37.1 %copy-start.6 = (u32[32]{0:T(128)S(1)}, u32[32]{0:T(128)}, u32[]{:S(2)}) copy-start(u32[32]{0:T(128)} %constant.10) | copy-start | bytes 388
  141.6 15.9 %all-to-all-start.1 = ((f32[4,96,576]{2,1,0:T(8,128)}), f32[4,96,576]{2,1,0:T(8,128)S(1)}, u32[]{:S(2)}, u32[]{:S(2)}) async-start(f32[4,96,576]{2,1,0:T(8,128)} %bitcast.17), calls=%async_computation.2 | async-start | bytes 1966080 | tf_op jit(solution)/shard_map/all_to_all | solution.py:35
  157.5 0.9 copy-start.4
  158.4 42.6 %copy-start.3 = (bf16[96,4,576]{2,0,1:T(8,128)(2,1)S(1)}, bf16[96,4,576]{2,0,1:T(8,128)(2,1)}, u32[]{:S(2)}) copy-start(bf16[96,4,576]{2,0,1:T(8,128)(2,1)} %copy-done.2) | copy-start | bytes 1327108
  196.7 11.4 %collective-permute-start = (f32[16,2304]{1,0:T(8,128)S(1)}, f32[16,2304]{1,0:T(8,128)S(1)}, u32[]{:S(2)}, u32[]{:S(2)}) collective-permute-start(f32[16,2304]{1,0:T(8,128)S(1)} %fusion), channel_id=1, source_target_pairs={{0,1},{1,2},{2,3},{3,4},{4,5},{5,6},{6,7},{8,9},{9,10},{10,11},{11... | collective-permute-start | bytes 442376
  198.6 9.5 %collective-permute-start.1 = (f32[12,2304]{1,0:T(8,128)S(1)}, f32[12,2304]{1,0:T(8,128)S(1)}, u32[]{:S(2)}, u32[]{:S(2)}) collective-permute-start(f32[12,2304]{1,0:T(8,128)S(1)} %slice), channel_id=1, source_target_pairs={{0,2},{1,3},{2,4},{3,5},{4,6},{5,7},{8,10},{9,11},{10,12},{11,13},... | collective-permute-start | bytes 331784
Sparse Core Ops, SparseCore 0:
  25.8 44.7 reduce-scatter.3
  108.1 29.6 all-gather.1
where the time goes:
time: 217 us; the launch traced here: 216 us
  waiting for transfers between devices  86.8 us (40%)
  blocking collectives  78.7 us (36%)
  between operations  14.8 us (7%)
  matrix products  11.9 us (5%)
  local copies, waits for them, and re-layouts  10.5 us (5%)
  starting transfers between devices  7.91 us (4%)
  other arithmetic  5.41 us (2%)
    reduce_scatter x1, waiting for transfers between devices, local(): lax.psum_scatter(lax.dot_general(width_part, embedding, (((1,), (1,)), ((...  43.8 us
    unnamed x1, blocking collectives  32.7 us
    all_gather x1, waiting for transfers between devices, local(): grad_piece = lax.all_gather(grads, 'layer', axis=0, tiled=True)  29.8 us
    pmax x1, blocking collectives, local(): lax.pmax((jnp.max(logits, axis=1), jnp.max(teach_f, axis=1)), ('row', 'co...  17.8 us
    psum x1, blocking collectives, local(): sum_s, sum_t = lax.psum((part_s, part_t), ('row', 'col'))  14.2 us
    all_to_all x1, blocking collectives, local(): lax.all_to_all(token_rows, 'layer', split_axis=1, concat_axis=0, tiled=True)  11.5 us
    all_to_all x1, waiting for transfers between devices, local(): lax.all_to_all(hidden_piece, 'layer', split_axis=0, concat_axis=1, tiled=...  11.2 us
    all_to_all x2, local copies, waits for them, and re-layouts, local(): lax.all_to_all(hidden_piece, 'layer', split_axis=0, concat_axis=1, tiled=...  5.53 us
  transfers between devices with their start and end apart: 5, of which 4 were waited for; matrix products, arithmetic and copies ran while one was open for 3% of the time, Pallas kernels for 0%

commit v1 on v0

--- a/solution.py
+++ b/solution.py
@@ -32,7 +32,12 @@
         grad_piece, width_part, (((0,), (0,)), ((), ())), preferred_element_type=jnp.float32
     )
     hidden_piece = jnp.dot(grad_piece, embedding, preferred_element_type=jnp.float32)
-    hidden_terms = lax.all_to_all(hidden_piece, "layer", split_axis=0, concat_axis=1, tiled=True)
+    hidden_terms = jnp.concatenate(
+        lax.all_to_all(
+            jnp.stack(jnp.split(hidden_piece, lax.axis_size("layer"), axis=0)), "layer", 0, 0
+        ),
+        axis=1,
+    )
     grad_hidden = lax.psum_scatter(hidden_terms, ("row", "col"), scatter_dimension=0, tiled=True)
     return (embed_acc, grad_hidden)
 

time: 217 us -> 215 us (level)
    all_to_all x2 -> x0, local copies, waits for them, and re-layouts: 5.53 us -> none  [local(): lax.all_to_all(hidden_piece, 'layer', split_axis=0, concat_axis=1, tiled=...]
    reshape x0 -> x2, local copies, waits for them, and re-layouts: none -> 4.37 us  [local(): jnp.concatenate(lax.all_to_all(jnp.stack(jnp.split(hidden_piece, lax.axis...]
where the time goes in v1:
time: 215 us
  waiting for transfers between devices  86.9 us (40%)
  blocking collectives  78.7 us (37%)
  between operations  14.8 us (7%)
  matrix products  10.9 us (5%)
  local copies, waits for them, and re-layouts  10 us (5%)
  starting transfers between devices  7.91 us (4%)
  other arithmetic  5.49 us (3%)
    reduce_scatter x1, waiting for transfers between devices, local(): lax.psum_scatter(lax.dot_general(width_part, embedding, (((1,), (1,)), ((...  43.8 us
    unnamed x1, blocking collectives  32.7 us
    all_gather x1, waiting for transfers between devices, local(): grad_piece = lax.all_gather(grads, 'layer', axis=0, tiled=True)  29.8 us
    pmax x1, blocking collectives, local(): lax.pmax((jnp.max(logits, axis=1), jnp.max(teach_f, axis=1)), ('row', 'co...  17.8 us
    psum x1, blocking collectives, local(): sum_s, sum_t = lax.psum((part_s, part_t), ('row', 'col'))  14.2 us
    all_to_all x1, blocking collectives, local(): lax.all_to_all(token_rows, 'layer', split_axis=1, concat_axis=0, tiled=True)  11.5 us
    all_to_all x1, waiting for transfers between devices, local(): lax.all_to_all(jnp.stack(jnp.split(hidden_piece, lax.axis_size('layer'),...  11.2 us
    dot_general x1, matrix products, local(): lax.dot_general(grad_piece, width_part, (((0,), (0,)), ((), ())), preferr...  5.03 us
  transfers between devices with their start and end apart: 5, of which 4 were waited for; matrix products, arithmetic and copies ran while one was open for 3% of the time, Pallas kernels for 0%

profile of v1, /device:TPU:1, one launch (start us, length us, event | category | flops | bytes accessed | tf_op | source)
XLA Modules:
  0.0 214.7 jit_solution(13435907915188764334)
XLA Ops:
  7.2 0.0 copy-start
  7.2 0.0 reduce-scatter.4.cloned.1.call-start
  7.2 2.5 %all_gather.6 = bf16[96,2304]{1,0:T(8,128)(2,1)S(1)} all-gather(bf16[48,2304]{1,0:T(8,128)(2,1)} %param.3), channel_id=1, replica_groups=mesh['layer'=4,'row'=2,'col'=4] {'row'}, dimensions={0}, use_global_device_ids=true | all-gather | bytes 663552 | tf_op jit(solution)/shard_map/all_gather | solution.py:10
  9.7 0.6 all_to_all.17
  10.3 0.1 copy.10
  10.3 11.5 %all_to_all.24 = bf16[96,4,576]{2,0,1:T(8,128)(2,1)S(1)} all-to-all(bf16[96,4,576]{2,0,1:T(8,128)(2,1)S(1)} %copy.10), channel_id=1, replica_groups=mesh['layer'=4,'row'=2,'col'=4] {'layer'}, dimensions={1} | all-to-all | bytes 884736 | tf_op jit(solution)/shard_map/all_to_all | solution.py:11
  21.8 0.0 copy-start.2
  21.8 0.8 copy-done.2
  22.6 0.0 copy-done
  22.6 3.1 %fusion.7 = f32[384,2048]{1,0:T(8,128)} fusion(bf16[384,576]{1,0:T(8,128)(2,1)S(1)} %bitcast.21, bf16[2048,576]{0,1:T(8,128)(2,1)S(1)} %copy-done), kind=kOutput, calls=%fused_computation.17 | convolution fusion | flops 905969664 | bytes 5947392 | tf_op jit(solution)/shard_map/dot_general | solution.py:13
  25.7 0.0 copy-start.4
  25.7 0.0 reduce-scatter.4.cloned.1.call-update
  25.7 0.0 all-gather.2.cloned.1.call-start
  25.8 0.9 copy-done.4
  26.7 0.2 reduce_max.24
  26.8 43.8 %reduce-scatter.4.cloned.1.call-done = f32[96,2048]{1,0:T(8,128)} async-done(((f32[384,2048]{1,0:T(8,128)}), f32[96,2048]{1,0:T(8,128)}) %reduce-scatter.4.cloned.1.call-update) | async-done | bytes 786448 | tf_op jit(solution)/shard_map/reduce_scatter | solution.py:12
  70.6 0.0 copy-start.1
  70.6 1.3 reduce_max.23
  72.0 17.8 %all-reduce.3 = (f32[96]{0:T(128)S(1)}, f32[96]{0:T(128)S(1)}) all-reduce(bf16[96]{0:T(256)(128)(2,1)S(1)} %reduce_max.24, f32[96]{0:T(128)S(1)} %reduce_max.23), channel_id=1, replica_groups=mesh['layer'=4,'row'=2,'col'=4] {'row','col'}, use_global_device_ids=true, to_apply=%region_6.0 | all-reduce | flops 192 | bytes 1344 | tf_op jit(solution)/shard_map/pmax | solution.py:21
  89.8 1.5 fusion.2
  91.4 14.2 %all-reduce.2 = (f32[96]{0:T(128)}, f32[96]{0:T(128)}) all-reduce(f32[96]{0:T(128)S(1)} %get-tuple-element.10, f32[96]{0:T(128)S(1)} %get-tuple-element.11), channel_id=1, replica_groups=mesh['layer'=4,'row'=2,'col'=4] {'row','col'}, use_global_device_ids=true, to_apply=%region_8.0 | all-reduce | flops 192 | bytes 1536 | tf_op jit(solution)/shard_map/psum | solution.py:24
  105.6 0.7 log_add_fusion
  106.2 0.7 log_add_fusion.1
  106.9 0.0 copy-done.1
  106.9 1.1 fusion.6
  108.0 0.0 all-gather.2.cloned.1.call-update
  108.0 29.8 %all-gather.2.cloned.1.call-done = bf16[384,2048]{1,0:T(8,128)(2,1)} async-done(((bf16[96,2048]{1,0:T(8,128)(2,1)}), bf16[384,2048]{1,0:T(8,128)(2,1)}) %all-gather.2.cloned.1.call-update) | async-done | bytes 1572880 | tf_op jit(solution)/shard_map/all_gather | solution.py:30
  137.8 2.8 %fusion.9 = f32[384,576]{0,1:T(8,128)S(1)} fusion(bf16[384,2048]{1,0:T(8,128)(2,1)} %all-gather.2.cloned.1.call-done, bf16[2048,576]{0,1:T(8,128)(2,1)S(1)} %copy-done), kind=kOutput, calls=%fused_computation.19 | convolution fusion | flops 905969664 | bytes 4816896 | tf_op jit(solution)/shard_map/dot_general | solution.py:34
  140.6 0.3 slice_bitcast_fusion.3
  140.9 0.1 pad_maximum_fusion
  141.0 0.0 copy-start.5
  141.0 1.3 copy.11
  142.3 3.5 %all-to-all-start.1 = ((f32[4,96,576]{2,1,0:T(8,128)}), f32[4,96,576]{2,1,0:T(8,128)S(1)}, u32[]{:S(2)}, u32[]{:S(2)}) async-start(f32[4,96,576]{2,1,0:T(8,128)} %copy.11), calls=%async_computation.2 | async-start | bytes 1966080 | tf_op jit(solution)/shard_map/all_to_all | solution.py:36
  145.8 0.0 copy-done.5
  145.9 0.6 dynamic-slice.4
  147.1 11.2 %all-to-all-done.1 = f32[4,96,576]{2,1,0:T(8,128)S(1)} async-done(((f32[4,96,576]{2,1,0:T(8,128)}), f32[4,96,576]{2,1,0:T(8,128)S(1)}, u32[]{:S(2)}, u32[]{:S(2)}) %all-to-all-start.1) | async-done | bytes 884768 | tf_op jit(solution)/shard_map/all_to_all | solution.py:36
  158.3 1.6 copy.12
  159.8 0.0 copy-start.3
  159.8 2.8 %reshape.18 = f32[96,2304]{1,0:T(8,128)} reshape(f32[96,4,576]{2,1,0:T(4,128)} %copy.12) | data formatting | bytes 1769472 | tf_op jit(solution)/shard_map/reshape | solution.py:35
  162.6 32.7 %fusion = f32[16,2304]{1,0:T(8,128)S(1)} fusion(f32[96,2304]{1,0:T(8,128)} %reshape.18), kind=kCustom, calls=%all-reduce-scatter | all-reduce-scatter fusion | flops 294913 | bytes 1032704
  195.4 1.9 collective-permute-start
  197.3 2.4 %collective-permute-start.1 = (f32[12,2304]{1,0:T(8,128)S(1)}, f32[12,2304]{1,0:T(8,128)S(1)}, u32[]{:S(2)}, u32[]{:S(2)}) collective-permute-start(f32[12,2304]{1,0:T(8,128)S(1)} %slice), channel_id=1, source_target_pairs={{0,2},{1,3},{2,4},{3,5},{4,6},{5,7},{8,10},{9,11},{10,12},{11,13},... | collective-permute-start | bytes 331784
  199.7 0.0 copy-done.3
  199.7 5.0 %fusion.8 = f32[2048,576]{0,1:T(8,128)} fusion(bf16[384,2048]{1,0:T(8,128)(2,1)} %all-gather.2.cloned.1.call-done, bf16[384,576]{1,0:T(8,128)(2,1)S(1)} %bitcast.22), kind=kOutput, calls=%fused_computation.18 | convolution fusion | flops 905969664 | bytes 6733824 | tf_op jit(solution)/shard_map/dot_general | solution.py:31
  204.7 2.0 collective-permute-done.1
  206.8 0.0 collective-permute-done
  206.8 0.4 concatenate
  207.2 0.7 constant_dynamic-slice_fusion
  (1 shorter events, 0.0 us)
Async XLA Ops:
  7.2 15.5 %copy-start = (bf16[2048,576]{0,1:T(8,128)(2,1)S(1)}, bf16[2048,576]{0,1:T(8,128)(2,1)}, u32[]{:S(2)}) copy-start(bf16[2048,576]{0,1:T(8,128)(2,1)} %param.4) | copy-start | bytes 7077892
  7.2 63.5 %reduce-scatter.4.cloned.1.call-start = ((), (), s32[]{:S(2)}) async-start(), calls=%async_computation.3 | async-start | bytes 3932160 | tf_op jit(solution)/shard_map/reduce_scatter | solution.py:12
  21.8 0.8 copy-start.2
  25.7 1.0 copy-start.4
  25.7 112.1 %all-gather.2.cloned.1.call-start = ((), (), s32[]{:S(2)}) async-start(), calls=%async_computation.4 | async-start | bytes 1966080 | tf_op jit(solution)/shard_map/all_gather | solution.py:30
  70.6 36.2 %copy-start.1 = (f32[96,2048]{1,0:T(8,128)S(1)}, f32[96,2048]{1,0:T(8,128)}, u32[]{:S(2)}) copy-start(f32[96,2048]{1,0:T(8,128)} %reduce-scatter.4.cloned.1.call-done) | copy-start | bytes 2359300
  141.0 4.9 %copy-start.5 = (u32[32]{0:T(128)S(1)}, u32[32]{0:T(128)}, u32[]{:S(2)}) copy-start(u32[32]{0:T(128)} %constant.10) | copy-start | bytes 388
  142.3 15.9 %all-to-all-start.1 = ((f32[4,96,576]{2,1,0:T(8,128)}), f32[4,96,576]{2,1,0:T(8,128)S(1)}, u32[]{:S(2)}, u32[]{:S(2)}) async-start(f32[4,96,576]{2,1,0:T(8,128)} %copy.11), calls=%async_computation.2 | async-start | bytes 1966080 | tf_op jit(solution)/shard_map/all_to_all | solution.py:36
  159.8 39.9 %copy-start.3 = (bf16[96,4,576]{2,0,1:T(8,128)(2,1)S(1)}, bf16[96,4,576]{2,0,1:T(8,128)(2,1)}, u32[]{:S(2)}) copy-start(bf16[96,4,576]{2,0,1:T(8,128)(2,1)} %copy-done.2) | copy-start | bytes 1327108
  195.4 11.4 %collective-permute-start = (f32[16,2304]{1,0:T(8,128)S(1)}, f32[16,2304]{1,0:T(8,128)S(1)}, u32[]{:S(2)}, u32[]{:S(2)}) collective-permute-start(f32[16,2304]{1,0:T(8,128)S(1)} %fusion), channel_id=1, source_target_pairs={{0,1},{1,2},{2,3},{3,4},{4,5},{5,6},{6,7},{8,9},{9,10},{10,11},{11... | collective-permute-start | bytes 442376
  197.3 9.5 %collective-permute-start.1 = (f32[12,2304]{1,0:T(8,128)S(1)}, f32[12,2304]{1,0:T(8,128)S(1)}, u32[]{:S(2)}, u32[]{:S(2)}) collective-permute-start(f32[12,2304]{1,0:T(8,128)S(1)} %slice), channel_id=1, source_target_pairs={{0,2},{1,3},{2,4},{3,5},{4,6},{5,7},{8,10},{9,11},{10,12},{11,13},... | collective-permute-start | bytes 331784
Sparse Core Ops, SparseCore 0:
  25.8 44.7 reduce-scatter.3
  108.1 29.6 all-gather.1
